TPU v7x, 32 devices: a whole 2x2x4 slice. The times are simulated.
32 devices in a mesh: groups: 2 (over y), rows: 4 (over z), keys: 2 (over x), heads: 2 (over core).
Axes of the slice: x: 2, y: 2, z: 4, core: 2. Of those that a mesh axis runs over, the one named last changes fastest.
Arguments:
- pair: bfloat16 [1024, 512, 128], P(('groups', 'rows'), 'keys'), parts along dimension 0, may hold values from -6 to 6
- seq_length: int32 [2], P('groups'), parts along dimension 0, may hold values from 257 to 512
- tile_counts: int32 [1024, 4], P(('groups', 'rows')), parts along dimension 0, may hold values from 0 to 128, as said below
- ln_gain: float32 [128], replicated, may hold values from 0.5 to 1.5
- w_query: bfloat16 [128, 128], P(None, 'heads'), may hold values from -8 to 8
- w_key: bfloat16 [128, 128], P(None, 'heads'), may hold values from -0.5 to 0.5
- w_value: bfloat16 [128, 128], P(None, 'heads'), may hold values from -0.5 to 0.5
- w_gate: bfloat16 [128, 128], P(None, 'heads'), may hold values from -0.5 to 0.5
- w_bias: bfloat16 [128, 4], P(None, 'heads'), may hold values from -1.5 to 1.5
- w_out: bfloat16 [128, 128], replicated, may hold values from -2 to 2
Outputs:
- update: bfloat16 [1024, 512, 128], P(('groups', 'rows'), ('keys', 'heads')), parts along dimension 0
There are 2 independent parts, one for each index of `groups`. A program takes and returns all parts, laid end to end along the dimension named above; an argument that names none is the same for every part. Nothing has to cross between parts.
Inputs may be any that keep to these rules, and one draw needn't show every extreme that they name: `tile_counts`: for each row and each tile of 128 keys, how many of the tile's leading keys are valid; some rows have no valid key at all.
All inputs are finite; a program needn't handle non-finite values.
Results may differ from a plain program's by a relative error of at most 0.03.
The roundings to bfloat16 on the way count: a program that leaves them out, or rounds other values in their place, can miss the bound.
Values may be sent and summed in bfloat16 or wider, within the bound.
A program may use at most 192 MiB of HBM per device.

v0:
```python
import jax
import jax.numpy as jnp
from jax import lax
from jax.sharding import PartitionSpec as P

HEAD_DIM = 32
TILE = 128


norm_epsilon = 1e-05
masked_score = -1e30


def layer_norm(values, gain):
    center = values - jnp.mean(values, axis=-1, keepdims=True)
    spread = jnp.mean(center * center, axis=-1, keepdims=True)
    return center * lax.rsqrt(spread + norm_epsilon) * gain


def finish(row_sum, weighted):
    denom = jnp.maximum(row_sum, 1.0)
    result = weighted / denom[..., None]
    rows_dev, heads_dev, cols_dev, depth = result.shape
    result = jnp.transpose(result, (0, 2, 1, 3)).reshape(rows_dev, cols_dev, heads_dev * depth)
    return result.astype(jnp.bfloat16)


def per_device(
    pair, seq_length, tile_counts, ln_gain, w_query, w_key, w_value, w_gate, w_bias, w_out
):
    rows_dev, cols_dev, channels = pair.shape
    key_groups = lax.axis_size("keys")
    length_all = cols_dev * key_groups
    heads_dev = w_bias.shape[1]
    width_dev = heads_dev * HEAD_DIM
    normed = layer_norm(pair.astype(jnp.float32), ln_gain).astype(jnp.bfloat16)
    flat = normed.reshape(rows_dev * cols_dev, channels)
    queries = (
        (jnp.dot(flat, w_query, preferred_element_type=jnp.float32) * HEAD_DIM ** (-0.5))
        .astype(jnp.bfloat16)
        .reshape(rows_dev, cols_dev, heads_dev, HEAD_DIM)
    )
    keys_local = (
        jnp.dot(flat, w_key, preferred_element_type=jnp.float32)
        .astype(jnp.bfloat16)
        .reshape(rows_dev, cols_dev, heads_dev, HEAD_DIM)
    )
    values_local = (
        jnp.dot(flat, w_value, preferred_element_type=jnp.float32)
        .astype(jnp.bfloat16)
        .reshape(rows_dev, cols_dev, heads_dev, HEAD_DIM)
    )
    gate_act = jax.nn.sigmoid(jnp.dot(flat, w_gate, preferred_element_type=jnp.float32)).reshape(
        rows_dev, cols_dev, width_dev
    )
    bias_local = jnp.einsum("rkc,ch->hrk", normed, w_bias, preferred_element_type=jnp.float32)
    bias_rows = lax.all_gather(bias_local.astype(jnp.bfloat16), "rows", axis=1, tiled=True).astype(
        bias_local.dtype
    )
    positions = jnp.arange(length_all, dtype=jnp.int32)
    allowed = (positions[None, :] < seq_length[0]) & (
        (positions % TILE)[None, :] < jnp.repeat(tile_counts, TILE, axis=1)
    )
    bias_turn = lax.all_to_all(
        bias_rows.astype(jnp.bfloat16), "keys", split_axis=1, concat_axis=2, tiled=True
    ).astype(bias_rows.dtype)
    initial = (
        jnp.full((rows_dev, heads_dev, cols_dev), masked_score, jnp.float32),
        jnp.zeros((rows_dev, heads_dev, cols_dev), jnp.float32),
        jnp.zeros((rows_dev, heads_dev, cols_dev, HEAD_DIM), jnp.float32),
    )
    piece_keys = lax.all_gather(keys_local, "keys", axis=1, tiled=True)
    piece_values = lax.all_gather(values_local, "keys", axis=1, tiled=True)

    def one_tile(tile_index, state):
        row_max, row_sum, weighted = state
        offset = tile_index * TILE
        key_tile = lax.dynamic_slice_in_dim(piece_keys, offset, TILE, 1)
        value_tile = lax.dynamic_slice_in_dim(piece_values, offset, TILE, 1)
        tile_bias = lax.dynamic_slice_in_dim(bias_turn, offset, TILE, 2)
        shown = lax.dynamic_slice_in_dim(allowed, offset, TILE, 1)[:, None, None, :]
        scores = (
            jnp.einsum("rjhd,rkhd->rhjk", queries, key_tile, preferred_element_type=jnp.float32)
            + tile_bias[None]
        )
        scores = jnp.where(shown, scores, masked_score)
        new_max = jnp.maximum(row_max, jnp.max(scores, axis=-1))
        weights = jnp.where(shown, jnp.exp(scores - new_max[..., None]), 0.0)
        rescale = jnp.exp(row_max - new_max)
        row_sum = row_sum * rescale + jnp.sum(weights, axis=-1)
        weighted = weighted * rescale[..., None] + jnp.einsum(
            "rhjk,rkhd->rhjd",
            weights.astype(jnp.bfloat16),
            value_tile,
            preferred_element_type=jnp.float32,
        )
        return (new_max, row_sum, weighted)

    row_max, row_sum, weighted = lax.fori_loop(0, piece_keys.shape[1] // TILE, one_tile, initial)
    attended = finish(row_sum, weighted)
    attended = lax.optimization_barrier(attended).astype(jnp.float32)
    gated = (gate_act * attended).astype(jnp.bfloat16)
    head_rank = lax.axis_index("heads")
    w_rows = lax.dynamic_slice_in_dim(w_out, head_rank * width_dev, width_dev, 0)
    partial_out = jnp.einsum("rkc,cd->rkd", gated, w_rows, preferred_element_type=jnp.float32)
    return lax.psum_scatter(
        partial_out.astype(jnp.bfloat16), "heads", scatter_dimension=1, tiled=True
    )


def solution(mesh):
    in_specs = (
        P(("groups", "rows"), "keys", None),
        P("groups"),
        P(("groups", "rows"), None),
        P(),
        P(None, "heads"),
        P(None, "heads"),
        P(None, "heads"),
        P(None, "heads"),
        P(None, "heads"),
        P(),
    )
    out_specs = P(("groups", "rows"), ("keys", "heads"), None)
    return jax.shard_map(
        per_device, mesh=mesh, in_specs=in_specs, out_specs=out_specs, check_vma=False
    )
```

profile of v0, /device:TPU:0, one launch (start us, length us, event | category | flops | bytes accessed | tf_op | source)
XLA Modules:
  0.0 505.1 jit_solution(12324241964965826432)
XLA Ops:
  6.5 5.8 %convert_reduce_fusion = f32[128,256]{1,0:T(8,128)S(1)} fusion(bf16[128,256,128]{2,1,0:T(8,128)(2,1)} %param.12), kind=kLoop, calls=%fused_computation.33 | loop fusion | flops 8355840 | bytes 8519680 | tf_op jit(solution)/shard_map/reduce_sum | solution.py:15
  12.4 10.9 %fusion.25 = f32[128,256]{1,0:T(8,128)S(1)} fusion(bf16[128,256,128]{2,1,0:T(8,128)(2,1)} %param.12, f32[128,256]{1,0:T(8,128)S(1)} %broadcast_multiply_fusion), kind=kLoop, calls=%fused_computation.36 | loop fusion | flops 16744448 | bytes 8650752 | tf_op jit(solution)/shard_map/reduce_sum | solution.py:16
  23.3 9.9 %fusion.27 = bf16[128,256,128]{2,1,0:T(8,128)(2,1)S(1)} fusion(bf16[128,256,128]{2,1,0:T(8,128)(2,1)S(1)} %bitcast.83, f32[128]{0:T(128)S(1)} %copy-done.9, f32[128,256]{1,0:T(8,128)S(1)} %add_rsqrt_fusion, f32[128,256]{1,0:T(8,128)S(1)} %broadcast_multiply_fusion), kind=kLoop, calls=%fused_computation.38 | loop fusion | flops 20971520 | bytes 17039872 | tf_op jit(solution)/shard_map/convert_element_type | solution.py:36
  45.3 6.4 %convolution_convert_fusion = bf16[32768,64]{0,1:T(8,128)(2,1)S(1)} fusion(bf16[32768,128]{1,0:T(8,128)(2,1)} %bitcast.79, bf16[128,64]{0,1:T(8,128)(2,1)S(1)} %copy-done.6), kind=kOutput, calls=%fused_computation.29 | convolution fusion | flops 538968064 | bytes 12599296 | tf_op jit(solution)/shard_map/dot_general | solution.py:49
  57.5 6.8 %fusion.30 = bf16[2,128,256]{2,0,1:T(2,128)(2,1)S(1)} fusion(bf16[128,256,128]{2,1,0:T(8,128)(2,1)} %copy-done.1, bf16[128,2]{0,1:T(2,128)(2,1)S(1)} %copy-done.10), kind=kOutput, calls=%fused_computation.44 | convolution fusion | flops 16842752 | bytes 8520192 | tf_op jit(solution)/shard_map/rkc,ch->hrk/dot_general | solution.py:56
  64.3 17.8 %all_gather.10 = bf16[2,512,256]{2,0,1:T(2,128)(2,1)} all-gather(bf16[2,128,256]{2,0,1:T(2,128)(2,1)S(1)} %fusion.30), channel_id=1, replica_groups=mesh['groups'=2,'rows'=4,'keys'=2,'heads'=2] {'rows'}, dimensions={1}, use_global_device_ids=true | all-gather | bytes 655360 | tf_op jit(solution)/shard_map/all_gather | solution.py:57
  86.5 8.3 %fusion.21 = bf16[32768,64]{0,1:T(8,128)(2,1)} fusion(bf16[32768,128]{1,0:T(8,128)(2,1)} %bitcast.80, bf16[128,64]{0,1:T(8,128)(2,1)S(1)} %copy-done.7), kind=kOutput, calls=%fused_computation.28 | convolution fusion | flops 541065216 | bytes 12599296 | tf_op jit(solution)/shard_map/dot_general | solution.py:39
  94.9 9.7 %fusion.22 = f32[32768,64]{0,1:T(8,128)} fusion(bf16[32768,128]{1,0:T(8,128)(2,1)} %bitcast.81, bf16[128,64]{0,1:T(8,128)(2,1)S(1)} %copy-done.11), kind=kOutput, calls=%fused_computation.31 | convolution fusion | flops 543162368 | bytes 16793600 | tf_op jit(solution)/shard_map/dot_general | solution.py:53
  113.8 43.7 %all-gather.3.cloned.1.call-done = bf16[128,512,2,32]{1,3,2,0:T(8,128)(2,1)} async-done(((bf16[128,256,2,32]{1,3,2,0:T(8,128)(2,1)}), bf16[128,512,2,32]{1,3,2,0:T(8,128)(2,1)}) %all-gather.3.cloned.1.call-update) | async-done | bytes 8388624 | tf_op jit(solution)/shard_map/all_gather | solution.py:72
  157.5 105.5 %all-gather.5.cloned.1.call-done = bf16[128,512,2,32]{1,3,2,0:T(8,128)(2,1)} async-done(((bf16[128,256,2,32]{1,3,2,0:T(8,128)(2,1)}), bf16[128,512,2,32]{1,3,2,0:T(8,128)(2,1)}) %all-gather.5.cloned.1.call-update) | async-done | bytes 8388624 | tf_op jit(solution)/shard_map/all_gather | solution.py:73
  263.1 208.6 %while.18 = (s32[]{:T(128)}, f32[128,2,256]{2,1,0:T(2,128)S(1)}, f32[128,2,256]{2,1,0:T(2,128)S(1)}, f32[128,2,256,32]{2,3,1,0:T(8,128)}, pred[128,512]{1,0:T(8,...) while((s32[]{:T(128)}, f32[128,2,256]{2,1,0:T(2,128)S(1)}, ...), condition=%wide.region_5.6_spmd.clone, body=%wide.region_2.5_spmd.clone.sunk | while | flops 1189412864 | bytes 198525168 | solution.py:99
  263.1 16.2 %fusion.60 = (f32[128,2,256]{2,1,0:T(2,128)S(1)}, f32[128,2,128,256]{3,2,1,0:T(8,128)}) fusion(f32[2,256,128]{1,2,0:T(8,128)S(1)} %constant_dynamic-slice_fusion.4, pred[128,128]{1,0:T(8,128)(4,1)S(1)} %constant_dynamic-slice_fusion.5, bf16[128,256,2,32]{1,3,2,0:T(8,128)(2,1)} %get-tuple-element.327, ...), kind=kOutput, calls=%fused_computation.3.clone.1 | convolution fusion | flops 561971200 | bytes 40386564 | tf_op jit(solution)/shard_map/while/body/eval_jaxpr/rjhd,rkhd->rhjk/dot_general | solution.py:83
  279.5 16.8 %fusion.62 = f32[128,2,256]{2,1,0:T(2,128)S(1)} fusion(f32[128,2,128,256]{3,2,1,0:T(8,128)} %get-tuple-element.292, f32[128,2,256]{2,1,0:T(2,128)S(1)} %fusion.61, f32[2,256,128]{1,2,0:T(8,128)S(1)} %constant_dynamic-slice_fusion.4, pred[128,128]{1,0:T(8,128)(4,1)S(1)} %constant_dynamic-slice_fusion.5), kind=kLoop, calls=%fused_computation.5.clone.1 | loop fusion | flops 41877504 | bytes 34357248 | tf_op jit(solution)/shard_map/while/body/eval_jaxpr/reduce_sum | solution.py:90
  296.9 15.0 %fusion.64 = f32[128,2,256,32]{2,3,1,0:T(8,128)S(1)} fusion(f32[128,2,256,32]{2,3,1,0:T(8,128)S(1)} %copy-done.2, f32[128,2,256]{2,1,0:T(2,128)S(1)} %get-tuple-element.294, pred[]{:T(512)S(6)} %compare.4, f32[128,2,128,256]{3,2,1,0:T(8,128)} %get-tuple-element.292, f32[128,2,256]{2,1,0:T(2,128)S(1)} %fusion.61, ...), kind=kOutput, calls=%fused_computation.9.clone.1 | convolution fusion | flops 585105408 | bytes 53231620 | tf_op jit(solution)/shard_map/while/body/eval_jaxpr/rhjk,rkhd->rhjd/dot_general | solution.py:91
  315.3 16.2 %fusion.60 = (f32[128,2,256]{2,1,0:T(2,128)S(1)}, f32[128,2,128,256]{3,2,1,0:T(8,128)}) fusion(f32[2,256,128]{1,2,0:T(8,128)S(1)} %constant_dynamic-slice_fusion.4, pred[128,128]{1,0:T(8,128)(4,1)S(1)} %constant_dynamic-slice_fusion.5, bf16[128,256,2,32]{1,3,2,0:T(8,128)(2,1)} %get-tuple-element.327, ...), kind=kOutput, calls=%fused_computation.3.clone.1 | convolution fusion | flops 561971200 | bytes 40386564 | tf_op jit(solution)/shard_map/while/body/eval_jaxpr/rjhd,rkhd->rhjk/dot_general | solution.py:83
  331.7 16.8 %fusion.62 = f32[128,2,256]{2,1,0:T(2,128)S(1)} fusion(f32[128,2,128,256]{3,2,1,0:T(8,128)} %get-tuple-element.292, f32[128,2,256]{2,1,0:T(2,128)S(1)} %fusion.61, f32[2,256,128]{1,2,0:T(8,128)S(1)} %constant_dynamic-slice_fusion.4, pred[128,128]{1,0:T(8,128)(4,1)S(1)} %constant_dynamic-slice_fusion.5), kind=kLoop, calls=%fused_computation.5.clone.1 | loop fusion | flops 41877504 | bytes 34357248 | tf_op jit(solution)/shard_map/while/body/eval_jaxpr/reduce_sum | solution.py:90
  349.0 15.0 %fusion.64 = f32[128,2,256,32]{2,3,1,0:T(8,128)S(1)} fusion(f32[128,2,256,32]{2,3,1,0:T(8,128)S(1)} %copy-done.2, f32[128,2,256]{2,1,0:T(2,128)S(1)} %get-tuple-element.294, pred[]{:T(512)S(6)} %compare.4, f32[128,2,128,256]{3,2,1,0:T(8,128)} %get-tuple-element.292, f32[128,2,256]{2,1,0:T(2,128)S(1)} %fusion.61, ...), kind=kOutput, calls=%fused_computation.9.clone.1 | convolution fusion | flops 585105408 | bytes 53231620 | tf_op jit(solution)/shard_map/while/body/eval_jaxpr/rhjk,rkhd->rhjd/dot_general | solution.py:91
  367.4 16.2 %fusion.60 = (f32[128,2,256]{2,1,0:T(2,128)S(1)}, f32[128,2,128,256]{3,2,1,0:T(8,128)}) fusion(f32[2,256,128]{1,2,0:T(8,128)S(1)} %constant_dynamic-slice_fusion.4, pred[128,128]{1,0:T(8,128)(4,1)S(1)} %constant_dynamic-slice_fusion.5, bf16[128,256,2,32]{1,3,2,0:T(8,128)(2,1)} %get-tuple-element.327, ...), kind=kOutput, calls=%fused_computation.3.clone.1 | convolution fusion | flops 561971200 | bytes 40386564 | tf_op jit(solution)/shard_map/while/body/eval_jaxpr/rjhd,rkhd->rhjk/dot_general | solution.py:83
  383.8 16.8 %fusion.62 = f32[128,2,256]{2,1,0:T(2,128)S(1)} fusion(f32[128,2,128,256]{3,2,1,0:T(8,128)} %get-tuple-element.292, f32[128,2,256]{2,1,0:T(2,128)S(1)} %fusion.61, f32[2,256,128]{1,2,0:T(8,128)S(1)} %constant_dynamic-slice_fusion.4, pred[128,128]{1,0:T(8,128)(4,1)S(1)} %constant_dynamic-slice_fusion.5), kind=kLoop, calls=%fused_computation.5.clone.1 | loop fusion | flops 41877504 | bytes 34357248 | tf_op jit(solution)/shard_map/while/body/eval_jaxpr/reduce_sum | solution.py:90
  401.2 15.0 %fusion.64 = f32[128,2,256,32]{2,3,1,0:T(8,128)S(1)} fusion(f32[128,2,256,32]{2,3,1,0:T(8,128)S(1)} %copy-done.2, f32[128,2,256]{2,1,0:T(2,128)S(1)} %get-tuple-element.294, pred[]{:T(512)S(6)} %compare.4, f32[128,2,128,256]{3,2,1,0:T(8,128)} %get-tuple-element.292, f32[128,2,256]{2,1,0:T(2,128)S(1)} %fusion.61, ...), kind=kOutput, calls=%fused_computation.9.clone.1 | convolution fusion | flops 585105408 | bytes 53231620 | tf_op jit(solution)/shard_map/while/body/eval_jaxpr/rhjk,rkhd->rhjd/dot_general | solution.py:91
  419.6 16.2 %fusion.60 = (f32[128,2,256]{2,1,0:T(2,128)S(1)}, f32[128,2,128,256]{3,2,1,0:T(8,128)}) fusion(f32[2,256,128]{1,2,0:T(8,128)S(1)} %constant_dynamic-slice_fusion.4, pred[128,128]{1,0:T(8,128)(4,1)S(1)} %constant_dynamic-slice_fusion.5, bf16[128,256,2,32]{1,3,2,0:T(8,128)(2,1)} %get-tuple-element.327, ...), kind=kOutput, calls=%fused_computation.3.clone.1 | convolution fusion | flops 561971200 | bytes 40386564 | tf_op jit(solution)/shard_map/while/body/eval_jaxpr/rjhd,rkhd->rhjk/dot_general | solution.py:83
  436.0 16.8 %fusion.62 = f32[128,2,256]{2,1,0:T(2,128)S(1)} fusion(f32[128,2,128,256]{3,2,1,0:T(8,128)} %get-tuple-element.292, f32[128,2,256]{2,1,0:T(2,128)S(1)} %fusion.61, f32[2,256,128]{1,2,0:T(8,128)S(1)} %constant_dynamic-slice_fusion.4, pred[128,128]{1,0:T(8,128)(4,1)S(1)} %constant_dynamic-slice_fusion.5), kind=kLoop, calls=%fused_computation.5.clone.1 | loop fusion | flops 41877504 | bytes 34357248 | tf_op jit(solution)/shard_map/while/body/eval_jaxpr/reduce_sum | solution.py:90
  453.4 15.0 %fusion.64 = f32[128,2,256,32]{2,3,1,0:T(8,128)S(1)} fusion(f32[128,2,256,32]{2,3,1,0:T(8,128)S(1)} %copy-done.2, f32[128,2,256]{2,1,0:T(2,128)S(1)} %get-tuple-element.294, pred[]{:T(512)S(6)} %compare.4, f32[128,2,128,256]{3,2,1,0:T(8,128)} %get-tuple-element.292, f32[128,2,256]{2,1,0:T(2,128)S(1)} %fusion.61, ...), kind=kOutput, calls=%fused_computation.9.clone.1 | convolution fusion | flops 585105408 | bytes 53231620 | tf_op jit(solution)/shard_map/while/body/eval_jaxpr/rhjk,rkhd->rhjd/dot_general | solution.py:91
  482.2 16.4 %reduce-scatter.2.cloned.1.call-done = bf16[128,128,128]{2,1,0:T(8,128)(2,1)} async-done(((bf16[128,256,128]{2,1,0:T(8,128)(2,1)}), bf16[128,128,128]{2,1,0:T(8,128)(2,1)}) %reduce-scatter.2.cloned.1.call-update) | async-done | bytes 4194320 | tf_op jit(solution)/shard_map/reduce_scatter | solution.py:106
  (91 shorter events, 57.5 us)
Async XLA Ops:
  6.5 470.3 %copy-start = (bf16[128,128]{1,0:T(8,128)(2,1)S(1)}, bf16[128,128]{1,0:T(8,128)(2,1)}, u32[]{:S(2)}) copy-start(bf16[128,128]{1,0:T(8,128)(2,1)} %param.21) | copy-start | bytes 98308
  6.5 16.8 %copy-start.9 = (f32[128]{0:T(128)S(1)}, f32[128]{0:T(128)}, u32[]{:S(2)}) copy-start(f32[128]{0:T(128)} %param.15) | copy-start | bytes 1540
  6.5 151.0 %all-gather.3.cloned.1.call-start = ((), (), s32[]{:S(2)}) async-start(), calls=%async_computation.2 | async-start | bytes 12582912 | tf_op jit(solution)/shard_map/all_gather | solution.py:72
  6.5 16.8 %slice-start = ((s8[8388608]{0:T(1024)(128)(4,1)}), s8[4194304]{0:T(1024)(128)(4,1)S(1)}, s32[]{:S(2)}) async-start(s8[8388608]{0:T(1024)(128)(4,1)} %bitcast.82), calls=%async_computation.5 | async-start | bytes 8388608
  12.4 10.9 %slice-start.1 = ((s8[8388608]{0:T(1024)(128)(4,1)}), s8[4194304]{0:T(1024)(128)(4,1)S(1)}, s32[]{:S(2)}) async-start(s8[8388608]{0:T(1024)(128)(4,1)} %bitcast.82), calls=%async_computation.6 | async-start | bytes 8388608
  23.3 13.2 %copy-start.5 = (bf16[128,64]{0,1:T(8,128)(2,1)S(1)}, bf16[128,64]{0,1:T(8,128)(2,1)}, u32[]{:S(2)}) copy-start(bf16[128,64]{0,1:T(8,128)(2,1)} %param.17) | copy-start | bytes 49156
  33.3 3.2 copy-start.1
  40.6 4.7 copy-start.6
  45.1 218.0 %all-gather.5.cloned.1.call-start = ((), (), s32[]{:S(2)}) async-start(), calls=%async_computation.3 | async-start | bytes 12582912 | tf_op jit(solution)/shard_map/all_gather | solution.py:73
  52.8 4.7 copy-start.10
  57.5 29.0 %copy-start.7 = (bf16[128,64]{0,1:T(8,128)(2,1)S(1)}, bf16[128,64]{0,1:T(8,128)(2,1)}, u32[]{:S(2)}) copy-start(bf16[128,64]{0,1:T(8,128)(2,1)} %param.16) | copy-start | bytes 49156
  64.3 30.6 %copy-start.11 = (bf16[128,64]{0,1:T(8,128)(2,1)S(1)}, bf16[128,64]{0,1:T(8,128)(2,1)}, u32[]{:S(2)}) copy-start(bf16[128,64]{0,1:T(8,128)(2,1)} %param.19) | copy-start | bytes 49156
  82.1 30.5 %all-to-all-start = ((bf16[2,512,256]{2,0,1:T(2,128)(2,1)}), bf16[2,512,256]{2,0,1:T(2,128)(2,1)S(1)}, u32[]{:S(2)}, u32[]{:S(2)}) async-start(bf16[2,512,256]{2,0,1:T(2,128)(2,1)} %all_gather.10), calls=%async_computation | async-start | bytes 1048576 | tf_op jit(solution)/shard_map/all_to_all | solution.py:64
  85.6 413.0 %reduce-scatter.2.cloned.1.call-start = ((), (), s32[]{:S(2)}) async-start(), calls=%async_computation.4 | async-start | bytes 12582912 | tf_op jit(solution)/shard_map/reduce_scatter | solution.py:106
  104.5 7.7 %copy-start.8 = (s32[128,4]{0,1:T(4,128)S(1)}, s32[128,4]{0,1:T(4,128)}, u32[]{:S(2)}) copy-start(s32[128,4]{0,1:T(4,128)} %param.14) | copy-start | bytes 6148
  279.5 17.4 %copy-start.2 = (f32[128,2,256,32]{2,3,1,0:T(8,128)S(1)}, f32[128,2,256,32]{2,3,1,0:T(8,128)}, u32[]{:S(2)}) copy-start(f32[128,2,256,32]{2,3,1,0:T(8,128)} %get-tuple-element.311) | copy-start | bytes 25165828 | tf_op jit(solution)/shard_map/while
  311.9 3.2 copy-start.3
  331.7 17.4 %copy-start.2 = (f32[128,2,256,32]{2,3,1,0:T(8,128)S(1)}, f32[128,2,256,32]{2,3,1,0:T(8,128)}, u32[]{:S(2)}) copy-start(f32[128,2,256,32]{2,3,1,0:T(8,128)} %get-tuple-element.311) | copy-start | bytes 25165828 | tf_op jit(solution)/shard_map/while
  364.1 3.2 copy-start.3
  383.8 17.4 %copy-start.2 = (f32[128,2,256,32]{2,3,1,0:T(8,128)S(1)}, f32[128,2,256,32]{2,3,1,0:T(8,128)}, u32[]{:S(2)}) copy-start(f32[128,2,256,32]{2,3,1,0:T(8,128)} %get-tuple-element.311) | copy-start | bytes 25165828 | tf_op jit(solution)/shard_map/while
  416.2 3.2 copy-start.3
  436.0 17.4 %copy-start.2 = (f32[128,2,256,32]{2,3,1,0:T(8,128)S(1)}, f32[128,2,256,32]{2,3,1,0:T(8,128)}, u32[]{:S(2)}) copy-start(f32[128,2,256,32]{2,3,1,0:T(8,128)} %get-tuple-element.311) | copy-start | bytes 25165828 | tf_op jit(solution)/shard_map/while
  468.4 3.2 copy-start.3
  471.8 5.8 %copy-start.4 = (f32[32768,64]{0,1:T(8,128)S(1)}, f32[32768,64]{0,1:T(8,128)}, u32[]{:S(2)}) copy-start(f32[32768,64]{0,1:T(8,128)} %fusion.22) | copy-start | bytes 25165828
Sparse Core Ops, SparseCore 0:
  45.2 112.2 all-gather.2
  159.1 103.9 all-gather.4
  482.3 16.2 reduce-scatter.1
where the time goes:
time: 506 us; the launch traced here: 505 us
  waiting for transfers between devices  166 us (33%)
  matrix products  164 us (32%)
  other arithmetic  102 us (20%)
  local copies, waits for them, and re-layouts  37.2 us (7%)
  blocking collectives  17.8 us (4%)
  between operations  14 us (3%)
    all_gather x1, waiting for transfers between devices, per_device(): piece_values = lax.all_gather(values_local, 'keys', axis=1, tiled=True)  106 us
    reduce_sum x4, other arithmetic, one_tile(): row_sum = row_sum * rescale + jnp.sum(weights, axis=-1)  67.2 us
    dot_general x4, matrix products, one_tile(): jnp.einsum('rjhd,rkhd->rhjk', queries, key_tile, preferred_element_type=j...  64.8 us
    dot_general x4, matrix products, one_tile(): jnp.einsum('rhjk,rkhd->rhjd', weights.astype(jnp.bfloat16), value_tile, p...  60.1 us
    all_gather x1, waiting for transfers between devices, per_device(): piece_keys = lax.all_gather(keys_local, 'keys', axis=1, tiled=True)  43.7 us
    all_gather x1, blocking collectives, per_device(): lax.all_gather(bias_local.astype(jnp.bfloat16), 'rows', axis=1, tiled=True)  17.8 us
    reduce_scatter x1, waiting for transfers between devices, per_device(): lax.psum_scatter(partial_out.astype(jnp.bfloat16), 'heads', scatter_dimen...  16.4 us
    unnamed x29, local copies, waits for them, and re-layouts  14 us
  transfers between devices with their start and end apart: 4, of which 3 were waited for; matrix products, arithmetic and copies ran while one was open for 9% of the time, Pallas kernels for 0%

commit v1 on v0

v1 whole, which is shorter than its diff:
```python
import functools

import jax
import jax.numpy as jnp
from jax import lax
from jax.experimental import pallas as pl
from jax.experimental.pallas import tpu as pltpu
from jax.sharding import PartitionSpec as P

HEAD_DIM = 32
TILE = 128
QUERY_TILE = 512
UNROLL = 1

norm_epsilon = 1e-05
masked_score = -1e30


def layer_norm(values, gain):
    center = values - jnp.mean(values, axis=-1, keepdims=True)
    spread = jnp.mean(center * center, axis=-1, keepdims=True)
    return center * lax.rsqrt(spread + norm_epsilon) * gain


def dot_nt(a, b):
    return lax.dot_general(a, b, (((1,), (1,)), ((), ())), preferred_element_type=jnp.float32)


def bias_kernel(_, pair_ref, gain_ref, w_ref, out_ref):
    rows, cols, channels = pair_ref.shape
    flat = pair_ref[...].reshape(rows * cols, channels).astype(jnp.float32)
    normed = layer_norm(flat, gain_ref[...]).astype(jnp.bfloat16)
    out_ref[...] = dot_nt(w_ref[...], normed).astype(jnp.bfloat16)


def pair_bias_part(pair, share, rows, gain, w_bias_t):
    _, cols, channels = pair.shape
    heads_pad = w_bias_t.shape[0]
    block = min(rows, 8)
    steps = rows // block
    return pl.pallas_call(
        bias_kernel,
        grid_spec=pltpu.PrefetchScalarGridSpec(
            num_scalar_prefetch=1,
            grid=(steps,),
            in_specs=[
                pl.BlockSpec((block, cols, channels), lambda r, which: (which[0] * steps + r, 0, 0)),
                pl.BlockSpec((1, channels), lambda r, which: (0, 0)),
                pl.BlockSpec((heads_pad, channels), lambda r, which: (0, 0)),
            ],
            out_specs=pl.BlockSpec((heads_pad, block * cols), lambda r, which: (0, r)),
        ),
        out_shape=jax.ShapeDtypeStruct((heads_pad, rows * cols), jnp.bfloat16),
        cost_estimate=pl.CostEstimate(
            flops=rows * cols * channels * 40, bytes_accessed=rows * cols * channels * 2,
            transcendentals=0,
        ),
        name="pair_bias",
    )(share, pair, gain, w_bias_t)


def attention_kernel(
    seq_ref, counts_ref, pair_ref, gain_ref, w_ref, w_out_ref, bias_ref, out_ref,
    query_s, key_s, value_s, gate_s, *, row_base,
):
    parts, _, cols, channels = pair_ref.shape
    length = parts * cols
    heads = bias_ref.shape[0]
    row = row_base + pl.program_id(0)
    seq_length = seq_ref[0]

    lane = lax.broadcasted_iota(jnp.int32, (TILE, channels), 1)
    depth = lax.broadcasted_iota(jnp.int32, (TILE, channels), 0)

    @pl.when(pl.program_id(0) == 0)
    def _():
        first_lane = jnp.where(lane == 0, 1.0, 0.0).astype(jnp.bfloat16)
        for t in range(length // TILE):
            query_s[t * TILE : (t + 1) * TILE, channels:] = first_lane

    flat = pair_ref[...].reshape(length, channels).astype(jnp.float32)
    normed = layer_norm(flat, gain_ref[...]).astype(jnp.bfloat16)
    projected = jnp.dot(normed, w_ref[...], preferred_element_type=jnp.float32)
    query_s[:, :channels] = (projected[:, :channels] * HEAD_DIM ** (-0.5)).astype(jnp.bfloat16)
    gate_s[...] = jax.nn.sigmoid(projected[:, 3 * channels :])
    for t in range(length // TILE):
        span = slice(t * TILE, (t + 1) * TILE)
        limit = jnp.minimum(counts_ref[row, t], seq_length - t * TILE)
        shown = depth < limit
        hidden = jnp.where(shown, 0.0, masked_score).astype(jnp.bfloat16)
        keys = projected[span, channels : 2 * channels]
        values = projected[span, 2 * channels : 3 * channels]
        for h in range(heads):
            mine = (lane >= h * HEAD_DIM) & (lane < (h + 1) * HEAD_DIM)
            both = mine & shown
            key_s[h, span, :channels] = jnp.where(mine, keys, 0.0).astype(jnp.bfloat16)
            key_s[h, span, channels:] = hidden
            value_s[h, span, :channels] = jnp.where(both, values, 0.0).astype(jnp.bfloat16)
            value_s[h, span, channels:] = jnp.where(both, 1.0, 0.0).astype(jnp.bfloat16)

    size = min(QUERY_TILE, length)
    out_cols = out_ref.shape[2]

    def one_tile(t, carry):
        start = pl.multiple_of(t * size, size)
        span = pl.ds(start, size)
        queries = query_s[span, :]
        total = None
        for h in range(heads):
            scores = dot_nt(queries, key_s[h]) + bias_ref[h, span, :].astype(jnp.float32)
            weights = jnp.exp(scores - jnp.max(scores, axis=-1, keepdims=True))
            term = jnp.dot(
                weights.astype(jnp.bfloat16), value_s[h], preferred_element_type=jnp.float32
            )
            total = term if total is None else total + term
        attended = total[:, :channels] / jnp.maximum(total[:, channels:], 1.0)
        attended = attended.astype(jnp.bfloat16).astype(jnp.float32)
        gated = (gate_s[span, :] * attended).astype(jnp.bfloat16)
        update = jnp.dot(gated, w_out_ref[...], preferred_element_type=jnp.float32)
        update = update.astype(jnp.bfloat16)
        ratio = size // out_cols
        for d in range(ratio):
            out_ref[t * ratio + d, 0] = update[d * out_cols : (d + 1) * out_cols]
        return carry

    lax.fori_loop(0, length // size, one_tile, 0, unroll=UNROLL)


def attention(
    seq_length, counts, pair, gain, weights, w_out, bias, row_base, first, rows, shards
):
    parts, _, cols, channels = pair.shape
    length = parts * cols
    heads = bias.shape[0]
    out_cols = length // shards
    whole = lambda *shape: pl.BlockSpec(
        shape, lambda r: (0,) * len(shape), pipeline_mode=pl.Buffered(1)
    )
    smem = pl.BlockSpec(memory_space=pltpu.SMEM)
    work = rows * heads * length * length
    return pl.pallas_call(
        functools.partial(attention_kernel, row_base=row_base),
        grid=(rows,),
        in_specs=[
            smem,
            smem,
            pl.BlockSpec((parts, 1, cols, channels), lambda r: (0, first + r, 0, 0)),
            whole(1, channels),
            whole(*weights.shape),
            whole(*w_out.shape),
            whole(*bias.shape),
        ],
        out_specs=pl.BlockSpec((shards, 1, out_cols, channels), lambda r: (0, r, 0, 0)),
        out_shape=jax.ShapeDtypeStruct((shards, rows, out_cols, channels), jnp.bfloat16),
        scratch_shapes=[
            pltpu.VMEM((length, 2 * channels), jnp.bfloat16),
            pltpu.VMEM((heads, length, 2 * channels), jnp.bfloat16),
            pltpu.VMEM((heads, length, 2 * channels), jnp.bfloat16),
            pltpu.VMEM((length, channels), jnp.float32),
        ],
        cost_estimate=pl.CostEstimate(
            flops=work * 1024, bytes_accessed=rows * length * channels * 4, transcendentals=work
        ),
        name="row_attention",
    )(seq_length, counts, pair, gain, weights, w_out, bias)


def chunk_sizes(rows):
    sizes = []
    left = rows
    while left > 1 and left > rows // 8:
        take = (left * 3 + 7) // 8
        sizes.append(take)
        left -= take
    return sizes + [left] if left else sizes


def per_device(
    pair, seq_length, tile_counts, ln_gain, w_query, w_key, w_value, w_gate, w_bias, w_out
):
    rows_dev, cols_dev, channels = pair.shape
    key_groups = lax.axis_size("keys")
    head_groups = lax.axis_size("heads")
    shards = key_groups * head_groups
    rows = rows_dev // shards
    heads_dev = w_bias.shape[1]
    heads = heads_dev * head_groups
    length = cols_dev * key_groups
    head_rank = lax.axis_index("heads")
    my_shard = lax.axis_index("keys") * head_groups + head_rank
    gain = ln_gain.reshape(1, channels)

    by_owner = pair.reshape(key_groups, head_groups, rows, cols_dev, channels)
    leaving = lax.dynamic_index_in_dim(by_owner, head_rank, 1, keepdims=False)
    arrived = lax.all_to_all(leaving, "keys", split_axis=0, concat_axis=0, tiled=True)
    counts = lax.dynamic_slice_in_dim(tile_counts, my_shard * rows, rows, 0)

    local = jnp.concatenate([w_query, w_key, w_value, w_gate, w_bias], axis=1)
    gathered = lax.all_gather(local, "heads", axis=0)
    width = w_query.shape[1]
    big = gathered[:, :, : 4 * width].reshape(head_groups, channels, 4, width)
    weights = jnp.transpose(big, (1, 2, 0, 3)).reshape(channels, 4 * width * head_groups)
    bias_t = jnp.transpose(gathered[:, :, 4 * width :], (0, 2, 1)).reshape(heads, channels)
    bias_t = jnp.pad(bias_t, ((0, -heads % 16), (0, 0)))

    share = rows_dev // head_groups
    rank = jnp.reshape(head_rank, (1,)).astype(jnp.int32)
    part = pair_bias_part(pair, rank, share, gain, bias_t)[:heads].reshape(heads, share, cols_dev)
    everyone = lax.all_gather(part, ("rows", "keys", "heads"), axis=0)
    everyone = everyone.reshape(-1, key_groups, head_groups, heads, share, cols_dev)
    bias = jnp.transpose(everyone, (3, 0, 2, 4, 1, 5)).reshape(heads, length, length)

    pieces = []
    done = 0
    for part in chunk_sizes(rows):
        update = attention(
            seq_length, counts, arrived, gain, weights, w_out, bias,
            done, done, part, shards,
        )
        done += part
        pieces.append(
            lax.all_to_all(update, ("keys", "heads"), split_axis=0, concat_axis=0, tiled=True)
        )
    return jnp.concatenate(pieces, axis=1).reshape(rows_dev, length // shards, channels)


def solution(mesh):
    in_specs = (
        P(("groups", "rows"), "keys", None),
        P("groups"),
        P(("groups", "rows"), None),
        P(),
        P(None, "heads"),
        P(None, "heads"),
        P(None, "heads"),
        P(None, "heads"),
        P(None, "heads"),
        P(),
    )
    out_specs = P(("groups", "rows"), ("keys", "heads"), None)
    return jax.shard_map(
        per_device, mesh=mesh, in_specs=in_specs, out_specs=out_specs, check_vma=False
    )
```

time: 506 us -> 235 us (0.46)
  matrix products: 164 us -> 0 us
  Pallas kernels: 0 us -> 111 us
  waiting for transfers between devices: 166 us -> 57.1 us
  other arithmetic: 102 us -> 0 us
  starting transfers between devices: 3.97 us -> 24 us
  blocking collectives: 17.8 us -> 2.06 us
  local copies, waits for them, and re-layouts: 37.2 us -> 25.8 us
    dot_general x14 -> x0, matrix products: 164 us -> none  [the longest x4 64.8 us: one_tile(): jnp.einsum('rjhd,rkhd->rhjk', queries, key_tile, preferred_element_type=j...]
    all_gather x2 -> x1, waiting for transfers between devices: 149 us -> 35.6 us  [per_device(): everyone = lax.all_gather(part, ('rows', 'keys', 'heads'), axis=0)]
    pallas_call x0 -> x6, Pallas kernels: none -> 111 us  [the longest x5 102 us: attention(): pl.pallas_call(functools.partial(attention_kernel, row_base=row_base), gr...]
    reduce_sum x6 -> x0, other arithmetic: 83.8 us -> none  [the longest x4 67.2 us: one_tile(): row_sum = row_sum * rescale + jnp.sum(weights, axis=-1)]
    all_to_all x1 -> x6, waiting for transfers between devices: 0.01 us -> 21.5 us  [the longest x5 10.9 us: per_device(): lax.all_to_all(update, ('keys', 'heads'), split_axis=0, concat_axis=0, ti...]
    all_to_all x1 -> x6, starting transfers between devices: 3.49 us -> 24 us  [the longest x5 18.3 us: per_device(): lax.all_to_all(update, ('keys', 'heads'), split_axis=0, concat_axis=0, ti...]
    reduce_scatter x1 -> x0, waiting for transfers between devices: 16.4 us -> none  [per_device(): lax.psum_scatter(partial_out.astype(jnp.bfloat16), 'heads', scatter_dimen...]
    all_gather x1, blocking collectives: 17.8 us -> 2.06 us  [per_device(): gathered = lax.all_gather(local, 'heads', axis=0)]
  transfers between devices with their start and end apart: 4 -> 7, of which waited for: 3 -> 4; matrix products, arithmetic and copies ran while one was open for 9% -> 7% of each run, Pallas kernels for 0% -> 39%
where the time goes in v1:
time: 235 us; the launch traced here: 234 us
  Pallas kernels  111 us (47%)
  waiting for transfers between devices  57.1 us (24%)
  local copies, waits for them, and re-layouts  25.8 us (11%)
  starting transfers between devices  24 us (10%)
  between operations  14.2 us (6%)
    pallas_call x5, Pallas kernels, attention(): pl.pallas_call(functools.partial(attention_kernel, row_base=row_base), gr...  102 us
    all_gather x1, waiting for transfers between devices, per_device(): everyone = lax.all_gather(part, ('rows', 'keys', 'heads'), axis=0)  35.6 us
    all_to_all x5, starting transfers between devices, per_device(): lax.all_to_all(update, ('keys', 'heads'), split_axis=0, concat_axis=0, ti...  18.3 us
    all_to_all x5, waiting for transfers between devices, per_device(): lax.all_to_all(update, ('keys', 'heads'), split_axis=0, concat_axis=0, ti...  10.9 us
    all_to_all x1, waiting for transfers between devices, per_device(): lax.all_to_all(leaving, 'keys', split_axis=0, concat_axis=0, tiled=True)  10.7 us
    unnamed x16, local copies, waits for them, and re-layouts  9.35 us
    pallas_call x1, Pallas kernels, pair_bias_part(): pl.pallas_call(bias_kernel, grid_spec=pltpu.PrefetchScalarGridSpec(num_sc...  8.78 us
    all_to_all x1, starting transfers between devices, per_device(): lax.all_to_all(leaving, 'keys', split_axis=0, concat_axis=0, tiled=True)  5.61 us
  transfers between devices with their start and end apart: 7, of which 4 were waited for; matrix products, arithmetic and copies ran while one was open for 7% of the time, Pallas kernels for 39%

profile of v1, /device:TPU:0, one launch (start us, length us, event | category | flops | bytes accessed | tf_op | source)
XLA Modules:
  0.0 234.1 jit_solution(10542403846756997666)
XLA Ops:
  10.1 2.1 all-gather
  12.9 8.8 %pair_bias.1 = bf16[16,16384]{1,0:T(8,128)(2,1)} custom-call(s32[1]{0:T(128)} %bitcast.6._, bf16[128,256,128]{2,1,0:T(8,128)(2,1)} %pair_ref.1, f32[1,128]{1,0:T(1,128)} %bitcast.31, bf16[16,128]{1,0:T(8,128)(2,1)} %pad.4.w_ref), custom_call_target="tpu_custom_call" | custom-call | flops 83886080 | bytes 4194304 | tf_op jit(solution)/shard_map/pair_bias/pallas_call | solution.py:41
  21.7 1.0 slice.14
  23.4 4.7 %dynamic-slice_bitcast_fusion = bf16[2,32,256,128]{3,2,1,0:T(8,128)(2,1)} fusion(bf16[2,2,32,256,128]{4,3,2,1,0:T(8,128)(2,1)} %bitcast.25, s32[]{:T(128)S(6)} %select_n.8), kind=kLoop, calls=%fused_computation | loop fusion | bytes 8388612 | tf_op jit(solution)/shard_map/jit(dynamic_index_in_dim)/squeeze | solution.py:194
  28.1 5.6 %all-to-all-start = ((bf16[2,32,256,128]{3,2,1,0:T(8,128)(2,1)}), bf16[2,32,256,128]{3,2,1,0:T(8,128)(2,1)}, u32[]{:S(2)}, u32[]{:S(2)}) async-start(bf16[2,32,256,128]{3,2,1,0:T(8,128)(2,1)} %dynamic-slice_bitcast_fusion), calls=%async_computation | async-start | bytes 8388608 | tf_op jit(solution)/shard_map/all_to_all | solution.py:195
  36.1 35.6 %all-gather.3.cloned.1.call-done = bf16[16,4,64,256]{3,2,1,0:T(8,128)(2,1)} async-done(((bf16[1,4,64,256]{3,2,1,0:T(8,128)(2,1)}), bf16[16,4,64,256]{3,2,1,0:T(8,128)(2,1)}) %all-gather.3.cloned.1.call-update) | async-done | bytes 2097168 | tf_op jit(solution)/shard_map/all_gather | solution.py:209
  71.6 3.8 %copy.39 = bf16[4,4,2,64,2,256]{5,4,3,2,1,0:T(2,128)(2,1)S(1)} copy(bf16[4,4,2,64,2,256]{5,3,0,2,4,1:T(8,128)(2,1)} %bitcast.26) | data formatting | bytes 4194304 | tf_op jit(solution)/shard_map/transpose | solution.py:211
  75.4 2.7 %reshape.34.bias_ref = bf16[4,512,512]{2,1,0:T(8,128)(2,1)} reshape(bf16[4,4,2,64,2,256]{5,4,3,2,1,0:T(2,128)(2,1)S(1)} %copy.39) | data formatting | bytes 4194304 | tf_op jit(solution)/shard_map/reshape | solution.py:211
  78.1 10.7 %all-to-all-done.pair_ref = bf16[2,32,256,128]{3,2,1,0:T(8,128)(2,1)} async-done(((bf16[2,32,256,128]{3,2,1,0:T(8,128)(2,1)}), bf16[2,32,256,128]{3,2,1,0:T(8,128)(2,1)}, u32[]{:S(2)}, u32[]{:S(2)}) %all-to-all-start) | async-done | bytes 4194336 | tf_op jit(solution)/shard_map/all_to_all | solution.py:195
  88.7 10.9 %row_attention.8 = bf16[4,3,128,128]{3,2,1,0:T(8,128)(2,1)} custom-call(s32[1]{0:T(128)S(6)} %copy.58.seq_ref, s32[32,4]{1,0:T(8,128)} %copy.45.counts_ref, bf16[2,32,256,128]{3,2,1,0:T(8,128)(2,1)} %all-to-all-done.pair_ref, f32[1,128]{1,0:T(1,128)} %bitcast.32, bf16[128,512]{1,0:T(8,128)(2,1)} %copy.40.w_ref, bf16[128,128]{1,0:T(8,128)(2,1)} %w_out_ref.9, ...), custom_call_target="tpu_custom_call" | custom-call | flops 3221225472 | bytes 786432 | tf_op jit(solution)/shard_map/row_attention/pallas_call | solution.py:141
  99.6 3.5 %all-to-all-start.4 = ((bf16[4,3,128,128]{3,2,1,0:T(8,128)(2,1)}), bf16[4,3,128,128]{3,2,1,0:T(8,128)(2,1)S(1)}, u32[]{:S(2)}, u32[]{:S(2)}) async-start(bf16[4,3,128,128]{3,2,1,0:T(8,128)(2,1)} %row_attention.8), calls=%async_computation.4 | async-start | bytes 786432 | tf_op jit(solution)/shard_map/all_to_all | solution.py:222
  103.1 16.5 %row_attention.7 = bf16[4,5,128,128]{3,2,1,0:T(8,128)(2,1)} custom-call(s32[1]{0:T(128)S(6)} %copy.58.seq_ref, s32[32,4]{1,0:T(8,128)} %copy.45.counts_ref, bf16[2,32,256,128]{3,2,1,0:T(8,128)(2,1)} %all-to-all-done.pair_ref, f32[1,128]{1,0:T(1,128)} %bitcast.33, bf16[128,512]{1,0:T(8,128)(2,1)} %copy.40.w_ref, bf16[128,128]{1,0:T(8,128)(2,1)} %w_out_ref.9, ...), custom_call_target="tpu_custom_call" | custom-call | flops 5368709120 | bytes 1310720 | tf_op jit(solution)/shard_map/row_attention/pallas_call | solution.py:141
  120.3 3.7 %all-to-all-start.3 = ((bf16[4,5,128,128]{3,2,1,0:T(8,128)(2,1)}), bf16[4,5,128,128]{3,2,1,0:T(8,128)(2,1)S(1)}, u32[]{:S(2)}, u32[]{:S(2)}) async-start(bf16[4,5,128,128]{3,2,1,0:T(8,128)(2,1)} %row_attention.7), calls=%async_computation.3 | async-start | bytes 1310720 | tf_op jit(solution)/shard_map/all_to_all | solution.py:222
  124.0 25.0 %row_attention.6 = bf16[4,8,128,128]{3,2,1,0:T(8,128)(2,1)} custom-call(s32[1]{0:T(128)S(6)} %copy.58.seq_ref, s32[32,4]{1,0:T(8,128)} %copy.45.counts_ref, bf16[2,32,256,128]{3,2,1,0:T(8,128)(2,1)} %all-to-all-done.pair_ref, f32[1,128]{1,0:T(1,128)} %bitcast.34, bf16[128,512]{1,0:T(8,128)(2,1)} %copy.40.w_ref, bf16[128,128]{1,0:T(8,128)(2,1)} %w_out_ref.9, ...), custom_call_target="tpu_custom_call" | custom-call | flops 8589934592 | bytes 2097152 | tf_op jit(solution)/shard_map/row_attention/pallas_call | solution.py:141
  149.0 3.5 %all-to-all-start.2 = ((bf16[4,8,128,128]{3,2,1,0:T(8,128)(2,1)}), bf16[4,8,128,128]{3,2,1,0:T(8,128)(2,1)S(1)}, u32[]{:S(2)}, u32[]{:S(2)}) async-start(bf16[4,8,128,128]{3,2,1,0:T(8,128)(2,1)} %row_attention.6), calls=%async_computation.2 | async-start | bytes 2097152 | tf_op jit(solution)/shard_map/all_to_all | solution.py:222
  152.5 36.2 %row_attention.5 = bf16[4,12,128,128]{3,2,1,0:T(8,128)(2,1)} custom-call(s32[1]{0:T(128)S(6)} %copy.58.seq_ref, s32[32,4]{1,0:T(8,128)} %copy.45.counts_ref, bf16[2,32,256,128]{3,2,1,0:T(8,128)(2,1)} %all-to-all-done.pair_ref, f32[1,128]{1,0:T(1,128)} %bitcast.35, bf16[128,512]{1,0:T(8,128)(2,1)} %copy.40.w_ref, bf16[128,128]{1,0:T(8,128)(2,1)} %w_out_ref.9, ...), custom_call_target="tpu_custom_call" | custom-call | flops 12884901888 | bytes 3145728 | tf_op jit(solution)/shard_map/row_attention/pallas_call | solution.py:141
  188.7 3.6 %all-to-all-start.1 = ((bf16[4,12,128,128]{3,2,1,0:T(8,128)(2,1)}), bf16[4,12,128,128]{3,2,1,0:T(8,128)(2,1)S(1)}, u32[]{:S(2)}, u32[]{:S(2)}) async-start(bf16[4,12,128,128]{3,2,1,0:T(8,128)(2,1)} %row_attention.5), calls=%async_computation.1 | async-start | bytes 3145728 | tf_op jit(solution)/shard_map/all_to_all | solution.py:222
  192.3 13.7 %row_attention.9 = bf16[4,4,128,128]{3,2,1,0:T(8,128)(2,1)} custom-call(s32[1]{0:T(128)S(6)} %copy.58.seq_ref, s32[32,4]{1,0:T(8,128)} %copy.45.counts_ref, bf16[2,32,256,128]{3,2,1,0:T(8,128)(2,1)} %all-to-all-done.pair_ref, f32[1,128]{1,0:T(1,128)} %bitcast.36, bf16[128,512]{1,0:T(8,128)(2,1)} %copy.40.w_ref, bf16[128,128]{1,0:T(8,128)(2,1)} %w_out_ref.9, ...), custom_call_target="tpu_custom_call" | custom-call | flops 4294967296 | bytes 1048576 | tf_op jit(solution)/shard_map/row_attention/pallas_call | solution.py:141
  206.0 6.3 %all-to-all-done.1 = bf16[4,12,128,128]{3,2,1,0:T(8,128)(2,1)S(1)} async-done(((bf16[4,12,128,128]{3,2,1,0:T(8,128)(2,1)}), bf16[4,12,128,128]{3,2,1,0:T(8,128)(2,1)S(1)}, u32[]{:S(2)}, u32[]{:S(2)}) %all-to-all-start.1) | async-done | bytes 1572896 | tf_op jit(solution)/shard_map/all_to_all | solution.py:222
  212.3 4.1 %all-to-all-start.5 = ((bf16[4,4,128,128]{3,2,1,0:T(8,128)(2,1)}), bf16[4,4,128,128]{3,2,1,0:T(8,128)(2,1)}, u32[]{:S(2)}, u32[]{:S(2)}) async-start(bf16[4,4,128,128]{3,2,1,0:T(8,128)(2,1)} %row_attention.9), calls=%async_computation.5 | async-start | bytes 1048576 | tf_op jit(solution)/shard_map/all_to_all | solution.py:222
  216.4 1.4 constant_dynamic-update-slice_fusion.9
  217.9 1.2 constant_dynamic-update-slice_fusion.8
  220.8 4.5 %all-to-all-done.5 = bf16[4,4,128,128]{3,2,1,0:T(8,128)(2,1)} async-done(((bf16[4,4,128,128]{3,2,1,0:T(8,128)(2,1)}), bf16[4,4,128,128]{3,2,1,0:T(8,128)(2,1)}, u32[]{:S(2)}, u32[]{:S(2)}) %all-to-all-start.5) | async-done | bytes 524320 | tf_op jit(solution)/shard_map/all_to_all | solution.py:222
  225.3 2.0 constant_dynamic-update-slice_fusion.5
  (29 shorter events, 9.2 us)
Async XLA Ops:
  6.5 27.9 %copy-start = (s32[128,4]{0,1:T(4,128)S(1)}, s32[128,4]{0,1:T(4,128)}, u32[]{:S(2)}) copy-start(s32[128,4]{0,1:T(4,128)} %param.12) | copy-start | bytes 6148
  6.5 65.1 %all-gather.3.cloned.1.call-start = ((), (), s32[]{:S(2)}) async-start(), calls=%async_computation.6 | async-start | bytes 2228224 | tf_op jit(solution)/shard_map/all_gather | solution.py:209
  28.1 60.7 %all-to-all-start = ((bf16[2,32,256,128]{3,2,1,0:T(8,128)(2,1)}), bf16[2,32,256,128]{3,2,1,0:T(8,128)(2,1)}, u32[]{:S(2)}, u32[]{:S(2)}) async-start(bf16[2,32,256,128]{3,2,1,0:T(8,128)(2,1)} %dynamic-slice_bitcast_fusion), calls=%async_computation | async-start | bytes 8388608 | tf_op jit(solution)/shard_map/all_to_all | solution.py:195
  99.6 20.0 %all-to-all-start.4 = ((bf16[4,3,128,128]{3,2,1,0:T(8,128)(2,1)}), bf16[4,3,128,128]{3,2,1,0:T(8,128)(2,1)S(1)}, u32[]{:S(2)}, u32[]{:S(2)}) async-start(bf16[4,3,128,128]{3,2,1,0:T(8,128)(2,1)} %row_attention.8), calls=%async_computation.4 | async-start | bytes 786432 | tf_op jit(solution)/shard_map/all_to_all | solution.py:222
  119.6 0.7 copy-start.1
  120.3 28.6 %all-to-all-start.3 = ((bf16[4,5,128,128]{3,2,1,0:T(8,128)(2,1)}), bf16[4,5,128,128]{3,2,1,0:T(8,128)(2,1)S(1)}, u32[]{:S(2)}, u32[]{:S(2)}) async-start(bf16[4,5,128,128]{3,2,1,0:T(8,128)(2,1)} %row_attention.7), calls=%async_computation.3 | async-start | bytes 1310720 | tf_op jit(solution)/shard_map/all_to_all | solution.py:222
  149.0 39.7 %all-to-all-start.2 = ((bf16[4,8,128,128]{3,2,1,0:T(8,128)(2,1)}), bf16[4,8,128,128]{3,2,1,0:T(8,128)(2,1)S(1)}, u32[]{:S(2)}, u32[]{:S(2)}) async-start(bf16[4,8,128,128]{3,2,1,0:T(8,128)(2,1)} %row_attention.6), calls=%async_computation.2 | async-start | bytes 2097152 | tf_op jit(solution)/shard_map/all_to_all | solution.py:222
  188.7 23.6 %all-to-all-start.1 = ((bf16[4,12,128,128]{3,2,1,0:T(8,128)(2,1)}), bf16[4,12,128,128]{3,2,1,0:T(8,128)(2,1)S(1)}, u32[]{:S(2)}, u32[]{:S(2)}) async-start(bf16[4,12,128,128]{3,2,1,0:T(8,128)(2,1)} %row_attention.5), calls=%async_computation.1 | async-start | bytes 3145728 | tf_op jit(solution)/shard_map/all_to_all | solution.py:222
  212.3 13.0 %all-to-all-start.5 = ((bf16[4,4,128,128]{3,2,1,0:T(8,128)(2,1)}), bf16[4,4,128,128]{3,2,1,0:T(8,128)(2,1)}, u32[]{:S(2)}, u32[]{:S(2)}) async-start(bf16[4,4,128,128]{3,2,1,0:T(8,128)(2,1)} %row_attention.9), calls=%async_computation.5 | async-start | bytes 1048576 | tf_op jit(solution)/shard_map/all_to_all | solution.py:222
  216.4 3.5 %copy-start.2 = (bf16[4,3,128,128]{3,2,1,0:T(8,128)(2,1)S(1)}, bf16[4,3,128,128]{3,2,1,0:T(8,128)(2,1)}, u32[]{:S(2)}) copy-start(bf16[4,3,128,128]{3,2,1,0:T(8,128)(2,1)} %copy-done.1) | copy-start | bytes 1179652
Sparse Core Ops, SparseCore 0:
  23.5 48.0 all-gather.2
